TPU v7x, 32 devices: a whole 2x2x4 slice. The times are simulated.
32 devices in a mesh: pr: 4 (over y, x), pc: 8 (over z, core).
Axes of the slice: x: 2, y: 2, z: 4, core: 2. Of those that a mesh axis runs over, the one named last changes fastest.
Arguments:
- pair_state: bfloat16 [96, 96, 128], P('pr', 'pc'), may hold values from -6 to 6
- left_weight: bfloat16 [128, 128], replicated, may hold values from -0.5 to 0.5
- right_weight: bfloat16 [128, 128], replicated, may hold values from -0.5 to 0.5
- mid_gain: float32 [128], replicated, may hold values from 0.25 to 1.75
- out_weight: bfloat16 [128, 128], replicated, may hold values from -0.5 to 0.5
- out_gate: bfloat16 [128, 128], replicated, may hold values from -0.5 to 0.5
Outputs:
- pair_update: bfloat16 [96, 96, 128], P('pr', 'pc')
All inputs are finite; a program needn't handle non-finite values.
Results may differ from a plain program's by a relative error of at most 0.012.
Values may be sent and summed in bfloat16 or wider, within the bound.
A program may use at most 128 MiB of HBM per device.

v0:
```python
import jax
import jax.numpy as jnp
from jax import lax
from jax.sharding import PartitionSpec as P


def scale_channels(values, channel_gain):
    centred = values - jnp.mean(values, axis=-1, keepdims=True)
    return (
        centred
        * lax.rsqrt(jnp.mean(centred * centred, axis=-1, keepdims=True) + 1e-05)
        * channel_gain
    )


def project_pair(pair_in, left_weight, right_weight):
    left = jnp.einsum("ijc,cd->ijd", pair_in, left_weight, preferred_element_type=jnp.float32)
    right = jnp.einsum("ijc,cd->ijd", pair_in, right_weight, preferred_element_type=jnp.float32)
    return (pair_in, left.astype(jnp.bfloat16), right.astype(jnp.bfloat16))


def close_update(mixed, ready, mid_gain, out_weight, out_gate):
    scaled = scale_channels(mixed.astype(jnp.float32), mid_gain).astype(jnp.bfloat16)
    scaled = lax.optimization_barrier(scaled)
    gate = jax.nn.sigmoid(
        jnp.einsum("ijc,cd->ijd", ready, out_gate, preferred_element_type=jnp.float32)
    )
    return (
        jnp.einsum("ijd,dc->ijc", scaled, out_weight, preferred_element_type=jnp.float32) * gate
    ).astype(jnp.bfloat16)


def body(pair_state, left_weight, right_weight, mid_gain, out_weight, out_gate):
    ready, left, right = project_pair(pair_state, left_weight, right_weight)
    count = pair_state.shape[0] * lax.axis_size("pr")
    left_lines, right_lines = (
        lax.all_to_all(left, "pr", split_axis=2, concat_axis=0, tiled=True),
        lax.all_to_all(right, "pr", split_axis=2, concat_axis=0, tiled=True),
    )
    strip = jnp.einsum(
        "kid,kjd->ijd",
        lax.all_gather(left_lines, "pc", axis=1, tiled=True),
        right_lines,
        preferred_element_type=jnp.float32,
    )
    strip = (strip * count ** (-0.5)).astype(jnp.bfloat16)
    mixed = lax.all_to_all(strip, "pr", split_axis=0, concat_axis=2, tiled=True)
    return close_update(mixed, ready, mid_gain, out_weight, out_gate)


def solution(mesh):
    placed = (P("pr", "pc", None), P(), P(), P(), P(), P())
    return jax.shard_map(
        body, mesh=mesh, in_specs=placed, out_specs=P("pr", "pc", None), check_vma=False
    )
```

profile of v0, /device:TPU:0, one launch (start us, length us, event | category | flops | bytes accessed | tf_op | source)
XLA Modules:
  0.0 52.5 jit_solution(6551884356601724737)
XLA Ops:
  0.0 0.9 %copy-done = bf16[24,12,128]{2,0,1:T(8,128)(2,1)S(1)} copy-done((bf16[24,12,128]{2,0,1:T(8,128)(2,1)S(1)}, bf16[24,12,128]{2,0,1:T(8,128)(2,1)}, u32[]{:S(2)}) %copy-start) | copy-done | bytes 73752
  0.9 0.9 %convolution_convert_fusion.1 = bf16[24,12,128]{2,0,1:T(8,128)(2,1)S(1)} fusion(bf16[24,12,128]{2,0,1:T(8,128)(2,1)S(1)} %copy-done, bf16[128,128]{1,0:T(8,128)(2,1)} %param.8), kind=kOutput, calls=%fused_computation.10 | convolution fusion | flops 9474048 | bytes 180224 | tf_op jit(solution)/shard_map/ijc,cd->ijd/dot_general | solution.py:18
  1.8 0.4 copy.39
  2.3 1.1 %reshape.28 = bf16[4,2,4608]{2,1,0:T(2,128)(2,1)} reshape(bf16[128,12,24]{2,1,0:T(8,128)(2,1)S(1)} %bitcast.44) | data formatting | bytes 147456
  3.4 5.3 %all-to-all-start = ((bf16[4,2,4608]{2,1,0:T(2,128)(2,1)}), bf16[4,2,4608]{2,1,0:T(2,128)(2,1)S(1)}, u32[]{:S(2)}, u32[]{:S(2)}) async-start(bf16[4,2,4608]{2,1,0:T(2,128)(2,1)} %reshape.28), calls=%async_computation | async-start | bytes 147456 | tf_op jit(solution)/shard_map/all_to_all | solution.py:38
  8.9 0.4 copy.41
  9.3 1.1 %reshape.26 = bf16[4,2,4608]{2,1,0:T(2,128)(2,1)} reshape(bf16[128,12,24]{2,1,0:T(8,128)(2,1)S(1)} %bitcast.45) | data formatting | bytes 147456
  10.5 3.1 %all-to-all-done = bf16[4,2,4608]{2,1,0:T(2,128)(2,1)S(1)} async-done(((bf16[4,2,4608]{2,1,0:T(2,128)(2,1)}), bf16[4,2,4608]{2,1,0:T(2,128)(2,1)S(1)}, u32[]{:S(2)}, u32[]{:S(2)}) %all-to-all-start) | async-done | bytes 73760 | tf_op jit(solution)/shard_map/all_to_all | solution.py:38
  13.6 3.3 %all-to-all-start.1 = ((bf16[4,2,4608]{2,1,0:T(2,128)(2,1)}), bf16[4,2,4608]{2,1,0:T(2,128)(2,1)S(1)}, u32[]{:S(2)}, u32[]{:S(2)}) async-start(bf16[4,2,4608]{2,1,0:T(2,128)(2,1)} %reshape.26), calls=%async_computation.1 | async-start | bytes 147456 | tf_op jit(solution)/shard_map/all_to_all | solution.py:37
  16.9 0.6 %reshape.29 = bf16[128,12,24]{2,1,0:T(8,128)(2,1)S(1)} reshape(bf16[4,2,4608]{2,1,0:T(2,128)(2,1)S(1)} %all-to-all-done) | data formatting | bytes 147456
  17.5 0.3 copy.55
  18.0 3.7 %all-to-all-done.1 = bf16[4,2,4608]{2,1,0:T(2,128)(2,1)S(1)} async-done(((bf16[4,2,4608]{2,1,0:T(2,128)(2,1)}), bf16[4,2,4608]{2,1,0:T(2,128)(2,1)S(1)}, u32[]{:S(2)}, u32[]{:S(2)}) %all-to-all-start.1) | async-done | bytes 73760 | tf_op jit(solution)/shard_map/all_to_all | solution.py:37
  21.7 0.6 %reshape.27 = bf16[128,12,24]{2,1,0:T(8,128)(2,1)S(1)} reshape(bf16[4,2,4608]{2,1,0:T(2,128)(2,1)S(1)} %all-to-all-done.1) | data formatting | bytes 147456
  22.3 0.3 copy.54
  22.9 16.5 %all_gather.3 = bf16[96,96,32]{0,2,1:T(8,128)(2,1)S(1)} all-gather(bf16[96,12,32]{0,2,1:T(8,128)(2,1)S(1)} %all_to_all.40), channel_id=1, replica_groups=mesh['pr'=4,'pc'=8] {'pc'}, dimensions={1}, use_global_device_ids=true | all-gather | bytes 663552 | tf_op jit(solution)/shard_map/all_gather | solution.py:42
  39.4 0.5 fusion.5
  39.9 0.4 copy.45
  40.3 0.3 reshape.30
  40.6 7.2 %all_to_all.45 = bf16[4,2,4608]{2,1,0:T(2,128)(2,1)S(1)} all-to-all(bf16[4,2,4608]{2,1,0:T(2,128)(2,1)S(1)} %reshape.30), channel_id=1, replica_groups=mesh['pr'=4,'pc'=8] {'pr'}, dimensions={0} | all-to-all | bytes 147456 | tf_op jit(solution)/shard_map/all_to_all | solution.py:47
  48.4 0.4 reshape.21
  49.8 0.4 copy-done.3
  50.3 0.6 %copy-done.2 = bf16[128,128]{1,0:T(8,128)(2,1)S(1)} copy-done((bf16[128,128]{1,0:T(8,128)(2,1)S(1)}, bf16[128,128]{1,0:T(8,128)(2,1)}, u32[]{:S(2)}) %copy-start.2) | copy-done | bytes 32792
  51.1 0.6 %copy-done.4 = bf16[128,128]{1,0:T(8,128)(2,1)S(1)} copy-done((bf16[128,128]{1,0:T(8,128)(2,1)S(1)}, bf16[128,128]{1,0:T(8,128)(2,1)}, u32[]{:S(2)}) %copy-start.4) | copy-done | bytes 32792
  51.7 0.8 %fusion.6 = bf16[24,12,128]{2,0,1:T(8,128)(2,1)} fusion(f32[24,12,128]{2,0,1:T(8,128)S(1)} %fusion.10, bf16[24,12,128]{2,0,1:T(8,128)(2,1)S(1)} %copy-done, bf16[128,128]{1,0:T(8,128)(2,1)S(1)} %copy-done.4), kind=kOutput, calls=%fused_computation.8 | convolution fusion | flops 9621504 | bytes 327680 | tf_op jit(solution)/shard_map/ijc,cd->ijd/dot_general | solution.py:26
  (19 shorter events, 2.4 us)
Async XLA Ops:
  0.0 0.9 %copy-start = (bf16[24,12,128]{2,0,1:T(8,128)(2,1)S(1)}, bf16[24,12,128]{2,0,1:T(8,128)(2,1)}, u32[]{:S(2)}) copy-start(bf16[24,12,128]{2,0,1:T(8,128)(2,1)} %param.6) | copy-start | bytes 221188
  3.4 5.3 %copy-start.1 = (bf16[128,128]{1,0:T(8,128)(2,1)S(1)}, bf16[128,128]{1,0:T(8,128)(2,1)}, u32[]{:S(2)}) copy-start(bf16[128,128]{1,0:T(8,128)(2,1)} %param.7) | copy-start | bytes 98308
  3.4 10.2 %all-to-all-start = ((bf16[4,2,4608]{2,1,0:T(2,128)(2,1)}), bf16[4,2,4608]{2,1,0:T(2,128)(2,1)S(1)}, u32[]{:S(2)}, u32[]{:S(2)}) async-start(bf16[4,2,4608]{2,1,0:T(2,128)(2,1)} %reshape.28), calls=%async_computation | async-start | bytes 147456 | tf_op jit(solution)/shard_map/all_to_all | solution.py:38
  13.6 8.1 %all-to-all-start.1 = ((bf16[4,2,4608]{2,1,0:T(2,128)(2,1)}), bf16[4,2,4608]{2,1,0:T(2,128)(2,1)S(1)}, u32[]{:S(2)}, u32[]{:S(2)}) async-start(bf16[4,2,4608]{2,1,0:T(2,128)(2,1)} %reshape.26), calls=%async_computation.1 | async-start | bytes 147456 | tf_op jit(solution)/shard_map/all_to_all | solution.py:37
  49.5 0.7 %copy-start.3 = (f32[128]{0:T(128)S(1)}, f32[128]{0:T(128)}, u32[]{:S(2)}) copy-start(f32[128]{0:T(128)} %param.9) | copy-start | bytes 1540
  50.2 0.8 %copy-start.2 = (bf16[128,128]{1,0:T(8,128)(2,1)S(1)}, bf16[128,128]{1,0:T(8,128)(2,1)}, u32[]{:S(2)}) copy-start(bf16[128,128]{1,0:T(8,128)(2,1)} %param.10) | copy-start | bytes 98308
  50.9 0.8 %copy-start.4 = (bf16[128,128]{1,0:T(8,128)(2,1)S(1)}, bf16[128,128]{1,0:T(8,128)(2,1)}, u32[]{:S(2)}) copy-start(bf16[128,128]{1,0:T(8,128)(2,1)} %param.11) | copy-start | bytes 98308
where the time goes:
time: 53.2 us; the launch traced here: 52.5 us
  blocking collectives  23.7 us (45%)
  local copies, waits for them, and re-layouts  10.1 us (19%)
  starting transfers between devices  8.61 us (16%)
  waiting for transfers between devices  6.78 us (13%)
  matrix products  2.61 us (5%)
  other arithmetic  0.54 us (1%)
    all_gather x1, blocking collectives, body(): lax.all_gather(left_lines, 'pc', axis=1, tiled=True)  16.5 us
    all_to_all x1, blocking collectives, body(): mixed = lax.all_to_all(strip, 'pr', split_axis=0, concat_axis=2, tiled=True)  7.24 us
    unnamed x16, local copies, waits for them, and re-layouts  6.51 us
    all_to_all x1, starting transfers between devices, body(): lax.all_to_all(right, 'pr', split_axis=2, concat_axis=0, tiled=True)  5.32 us
    all_to_all x1, waiting for transfers between devices, body(): lax.all_to_all(left, 'pr', split_axis=2, concat_axis=0, tiled=True)  3.68 us
    all_to_all x1, starting transfers between devices, body(): lax.all_to_all(left, 'pr', split_axis=2, concat_axis=0, tiled=True)  3.29 us
    all_to_all x1, waiting for transfers between devices, body(): lax.all_to_all(right, 'pr', split_axis=2, concat_axis=0, tiled=True)  3.1 us
  transfers between devices with their start and end apart: 2, of which 2 were waited for; matrix products, arithmetic and copies ran while one was open for 5% of the time, Pallas kernels for 0%

commit v1 on v0

--- a/solution.py
+++ b/solution.py
@@ -35,7 +35,10 @@
     count = pair_state.shape[0] * lax.axis_size("pr")
     left_lines, right_lines = (
         lax.all_to_all(left, "pr", split_axis=2, concat_axis=0, tiled=True),
-        lax.all_to_all(right, "pr", split_axis=2, concat_axis=0, tiled=True),
+        jnp.concatenate(
+            lax.all_to_all(jnp.stack(jnp.split(right, lax.axis_size("pr"), axis=2)), "pr", 0, 0),
+            axis=0,
+        ),
     )
     strip = jnp.einsum(
         "kid,kjd->ijd",

time: 53.2 us -> 52.7 us (level)
  local copies, waits for them, and re-layouts: 10.1 us -> 9.13 us
    unnamed x16, local copies, waits for them, and re-layouts: 6.51 us -> 5.84 us
    reshape x0 -> x2, local copies, waits for them, and re-layouts: none -> 0.58 us  [body(): jnp.concatenate(lax.all_to_all(jnp.stack(jnp.split(right, lax.axis_size('...]
where the time goes in v1:
time: 52.7 us; the launch traced here: 52 us
  blocking collectives  23.7 us (45%)
  local copies, waits for them, and re-layouts  9.13 us (17%)
  starting transfers between devices  8.61 us (16%)
  waiting for transfers between devices  7.15 us (14%)
  matrix products  2.61 us (5%)
  other arithmetic  0.63 us (1%)
    all_gather x1, blocking collectives, body(): lax.all_gather(left_lines, 'pc', axis=1, tiled=True)  16.5 us
    all_to_all x1, blocking collectives, body(): mixed = lax.all_to_all(strip, 'pr', split_axis=0, concat_axis=2, tiled=True)  7.24 us
    unnamed x16, local copies, waits for them, and re-layouts  5.84 us
    all_to_all x1, starting transfers between devices, body(): lax.all_to_all(jnp.stack(jnp.split(right, lax.axis_size('pr'), axis=2)),...  5.32 us
    all_to_all x1, waiting for transfers between devices, body(): lax.all_to_all(left, 'pr', split_axis=2, concat_axis=0, tiled=True)  4.04 us
    all_to_all x1, starting transfers between devices, body(): lax.all_to_all(left, 'pr', split_axis=2, concat_axis=0, tiled=True)  3.29 us
    all_to_all x1, waiting for transfers between devices, body(): lax.all_to_all(jnp.stack(jnp.split(right, lax.axis_size('pr'), axis=2)),...  3.11 us
  transfers between devices with their start and end apart: 2, of which 2 were waited for; matrix products, arithmetic and copies ran while one was open for 5% of the time, Pallas kernels for 0%

profile of v1, /device:TPU:0, one launch (start us, length us, event | category | flops | bytes accessed | tf_op | source)
XLA Modules:
  0.0 52.0 jit_solution(6563115257097415228)
XLA Ops:
  0.0 0.9 %copy-done = bf16[24,12,128]{2,0,1:T(8,128)(2,1)S(1)} copy-done((bf16[24,12,128]{2,0,1:T(8,128)(2,1)S(1)}, bf16[24,12,128]{2,0,1:T(8,128)(2,1)}, u32[]{:S(2)}) %copy-start) | copy-done | bytes 73752
  0.9 0.9 %convolution_convert_fusion.1 = bf16[24,12,128]{2,0,1:T(8,128)(2,1)S(1)} fusion(bf16[24,12,128]{2,0,1:T(8,128)(2,1)S(1)} %copy-done, bf16[128,128]{1,0:T(8,128)(2,1)} %param.8), kind=kOutput, calls=%fused_computation.10 | convolution fusion | flops 9474048 | bytes 180224 | tf_op jit(solution)/shard_map/ijc,cd->ijd/dot_general | solution.py:18
  2.0 0.9 %reshape.31 = bf16[4,2,4608]{2,1,0:T(2,128)(2,1)} reshape(bf16[4,12,24,32]{3,2,1,0:T(8,128)(2,1)S(1)} %fusion.13) | data formatting | bytes 147456
  2.9 5.3 %all-to-all-start = ((bf16[4,2,4608]{2,1,0:T(2,128)(2,1)}), bf16[4,2,4608]{2,1,0:T(2,128)(2,1)S(1)}, u32[]{:S(2)}, u32[]{:S(2)}) async-start(bf16[4,2,4608]{2,1,0:T(2,128)(2,1)} %reshape.31), calls=%async_computation | async-start | bytes 147456 | tf_op jit(solution)/shard_map/all_to_all | solution.py:39
  8.4 0.4 copy.37
  8.9 1.1 %reshape.33 = bf16[4,2,4608]{2,1,0:T(2,128)(2,1)} reshape(bf16[128,12,24]{2,1,0:T(8,128)(2,1)S(1)} %bitcast.49) | data formatting | bytes 147456
  10.0 3.1 %all-to-all-done = bf16[4,2,4608]{2,1,0:T(2,128)(2,1)S(1)} async-done(((bf16[4,2,4608]{2,1,0:T(2,128)(2,1)}), bf16[4,2,4608]{2,1,0:T(2,128)(2,1)S(1)}, u32[]{:S(2)}, u32[]{:S(2)}) %all-to-all-start) | async-done | bytes 73760 | tf_op jit(solution)/shard_map/all_to_all | solution.py:39
  13.1 3.3 %all-to-all-start.1 = ((bf16[4,2,4608]{2,1,0:T(2,128)(2,1)}), bf16[4,2,4608]{2,1,0:T(2,128)(2,1)S(1)}, u32[]{:S(2)}, u32[]{:S(2)}) async-start(bf16[4,2,4608]{2,1,0:T(2,128)(2,1)} %reshape.33), calls=%async_computation.1 | async-start | bytes 147456 | tf_op jit(solution)/shard_map/all_to_all | solution.py:37
  16.6 0.4 copy.44
  17.2 4.0 %all-to-all-done.1 = bf16[4,2,4608]{2,1,0:T(2,128)(2,1)S(1)} async-done(((bf16[4,2,4608]{2,1,0:T(2,128)(2,1)}), bf16[4,2,4608]{2,1,0:T(2,128)(2,1)S(1)}, u32[]{:S(2)}, u32[]{:S(2)}) %all-to-all-start.1) | async-done | bytes 73760 | tf_op jit(solution)/shard_map/all_to_all | solution.py:37
  21.3 0.6 %reshape.34 = bf16[128,12,24]{2,1,0:T(8,128)(2,1)S(1)} reshape(bf16[4,2,4608]{2,1,0:T(2,128)(2,1)S(1)} %all-to-all-done.1) | data formatting | bytes 147456
  21.9 0.3 copy.49
  22.4 16.5 %all_gather.3 = bf16[96,96,32]{0,2,1:T(8,128)(2,1)S(1)} all-gather(bf16[96,12,32]{0,2,1:T(8,128)(2,1)S(1)} %all_to_all.27), channel_id=1, replica_groups=mesh['pr'=4,'pc'=8] {'pc'}, dimensions={1}, use_global_device_ids=true | all-gather | bytes 663552 | tf_op jit(solution)/shard_map/all_gather | solution.py:45
  38.9 0.5 fusion.5
  39.4 0.4 copy.41
  39.8 0.3 reshape.35
  40.1 7.2 %all_to_all.32 = bf16[4,2,4608]{2,1,0:T(2,128)(2,1)S(1)} all-to-all(bf16[4,2,4608]{2,1,0:T(2,128)(2,1)S(1)} %reshape.35), channel_id=1, replica_groups=mesh['pr'=4,'pc'=8] {'pr'}, dimensions={0} | all-to-all | bytes 147456 | tf_op jit(solution)/shard_map/all_to_all | solution.py:50
  47.6 0.3 copy.42
  47.9 0.4 reshape.25
  48.7 0.3 copy.43
  49.3 0.4 copy-done.3
  49.8 0.6 %copy-done.2 = bf16[128,128]{1,0:T(8,128)(2,1)S(1)} copy-done((bf16[128,128]{1,0:T(8,128)(2,1)S(1)}, bf16[128,128]{1,0:T(8,128)(2,1)}, u32[]{:S(2)}) %copy-start.2) | copy-done | bytes 32792
  50.6 0.6 %copy-done.4 = bf16[128,128]{1,0:T(8,128)(2,1)S(1)} copy-done((bf16[128,128]{1,0:T(8,128)(2,1)S(1)}, bf16[128,128]{1,0:T(8,128)(2,1)}, u32[]{:S(2)}) %copy-start.4) | copy-done | bytes 32792
  51.2 0.8 %fusion.6 = bf16[24,12,128]{2,0,1:T(8,128)(2,1)} fusion(f32[24,12,128]{2,0,1:T(8,128)S(1)} %fusion.9, bf16[24,12,128]{2,0,1:T(8,128)(2,1)S(1)} %copy-done, bf16[128,128]{1,0:T(8,128)(2,1)S(1)} %copy-done.4), kind=kOutput, calls=%fused_computation.8 | convolution fusion | flops 9621504 | bytes 327680 | tf_op jit(solution)/shard_map/ijc,cd->ijd/dot_general | solution.py:26
  (20 shorter events, 2.2 us)
Async XLA Ops:
  0.0 0.9 %copy-start = (bf16[24,12,128]{2,0,1:T(8,128)(2,1)S(1)}, bf16[24,12,128]{2,0,1:T(8,128)(2,1)}, u32[]{:S(2)}) copy-start(bf16[24,12,128]{2,0,1:T(8,128)(2,1)} %param.6) | copy-start | bytes 221188
  2.9 5.3 %copy-start.1 = (bf16[128,128]{1,0:T(8,128)(2,1)S(1)}, bf16[128,128]{1,0:T(8,128)(2,1)}, u32[]{:S(2)}) copy-start(bf16[128,128]{1,0:T(8,128)(2,1)} %param.7) | copy-start | bytes 98308
  2.9 10.2 %all-to-all-start = ((bf16[4,2,4608]{2,1,0:T(2,128)(2,1)}), bf16[4,2,4608]{2,1,0:T(2,128)(2,1)S(1)}, u32[]{:S(2)}, u32[]{:S(2)}) async-start(bf16[4,2,4608]{2,1,0:T(2,128)(2,1)} %reshape.31), calls=%async_computation | async-start | bytes 147456 | tf_op jit(solution)/shard_map/all_to_all | solution.py:39
  13.1 8.1 %all-to-all-start.1 = ((bf16[4,2,4608]{2,1,0:T(2,128)(2,1)}), bf16[4,2,4608]{2,1,0:T(2,128)(2,1)S(1)}, u32[]{:S(2)}, u32[]{:S(2)}) async-start(bf16[4,2,4608]{2,1,0:T(2,128)(2,1)} %reshape.33), calls=%async_computation.1 | async-start | bytes 147456 | tf_op jit(solution)/shard_map/all_to_all | solution.py:37
  49.0 0.7 %copy-start.3 = (f32[128]{0:T(128)S(1)}, f32[128]{0:T(128)}, u32[]{:S(2)}) copy-start(f32[128]{0:T(128)} %param.9) | copy-start | bytes 1540
  49.7 0.8 %copy-start.2 = (bf16[128,128]{1,0:T(8,128)(2,1)S(1)}, bf16[128,128]{1,0:T(8,128)(2,1)}, u32[]{:S(2)}) copy-start(bf16[128,128]{1,0:T(8,128)(2,1)} %param.10) | copy-start | bytes 98308
  50.4 0.8 %copy-start.4 = (bf16[128,128]{1,0:T(8,128)(2,1)S(1)}, bf16[128,128]{1,0:T(8,128)(2,1)}, u32[]{:S(2)}) copy-start(bf16[128,128]{1,0:T(8,128)(2,1)} %param.11) | copy-start | bytes 98308
